TPU v7x, 256 devices: a whole 4x4x8 slice. The times are simulated.
256 devices in a mesh: grp: 32 (over z, y), rep: 8 (over x, core).
Axes of the slice: x: 4, y: 4, z: 8, core: 2. Of those that a mesh axis runs over, the one named last changes fastest.
Arguments:
- queries: bfloat16 [64, 8, 32, 128], P('grp', 'rep'), may hold values from -3.2 to 3.2
- passages: bfloat16 [2048, 8, 180, 128], P('grp', 'rep'), may hold values from -1.796875 to 1.796875
- lengths: int32 [2048, 8], P('grp', 'rep'), may hold values from 16 to 180
- cand_ids: int32 [64, 8, 64], P('grp', 'rep'), may hold values from 0 to 2047, as said below
- owner_map: int32 [8, 2048], P('rep'), may hold values from 0 to 2047, as said below
- teacher: float32 [64, 8, 64], P('grp', 'rep'), may hold values from -12 to 312
- weights: float32 [64, 8], P('grp', 'rep'), may hold values from 0.5 to 18
Outputs:
- loss: float32 [], replicated
- query_grad: float32 [64, 8, 32, 128], P('grp', 'rep')
- passage_grad: bfloat16 [2048, 8, 180, 128], P('grp', 'rep')
Inputs may be any that keep to these rules, and one draw needn't show every extreme that they name: `cand_ids`: within each replica, the 128 candidates of the queries of one grp index have storage rows of which at most 8 (counted with repeats) lie in any one aligned block of 64 rows; in every draw, in each replica, one block receives exactly 8 from every grp index. `owner_map`: each row is a permutation of 0 to 2047.
All inputs are finite; a program needn't handle non-finite values.
Results may differ from a plain program's by a relative error of at most 0.0055.
Values may be sent and summed in bfloat16 or wider, within the bound.
A program may use at most 128 MiB of HBM per device.

v0:
```python
import jax
import jax.numpy as jnp
from jax import lax
from jax.sharding import Mesh
from jax.sharding import PartitionSpec as P

GRP = ("grp_0", "grp_1")
REP = ("rep_0", "rep_1")
GRP_REP = ("grp_0", "grp_1", "rep_0", "rep_1")
temper = 0.05


def over_axes(shard, axes):
    for axis in axes:
        shard = lax.psum(shard, axis)
    return shard


def token_softmax(products, lengths_used):
    usable = (
        lax.broadcasted_iota(jnp.int32, products.shape, products.ndim - 1)
        < lengths_used[..., None, None]
    )
    scaled = jnp.where(usable, products / temper, -1e30)
    highest = jnp.max(scaled, axis=-1, keepdims=True)
    powers = jnp.where(usable, jnp.exp(scaled - highest), 0.0)
    summed = jnp.sum(powers, axis=-1, keepdims=True)
    matched = temper * (highest[..., 0] + jnp.log(summed[..., 0]))
    return (matched, powers / summed)


def on_device(queries, passages, lengths, cand_ids, owner_map, teacher, weights):
    groups = lax.axis_size(GRP)
    replicas = lax.axis_size(REP)
    query_local = queries.shape[0]
    query_len = queries.shape[2]
    feature_dim = queries.shape[3]
    passage_local = passages.shape[0]
    token_len = passages.shape[2]
    candidates = cand_ids.shape[2]
    ref_count = query_local * candidates
    capacity = 2 * ref_count // groups
    slot_count = groups * capacity
    block_width = token_len * feature_dim
    query_width = query_len * feature_dim
    position_table = owner_map[0]
    wanted = cand_ids[:, 0, :].reshape(ref_count)
    table_index = jnp.arange(position_table.shape[0], dtype=jnp.int32)
    positions = jnp.sum(
        jnp.where(wanted[:, None] == table_index[None, :], position_table[None, :], 0), axis=1
    )
    owner_index = positions // passage_local
    local_row = positions % passage_local
    owner_hot = (owner_index[:, None] == jnp.arange(groups, dtype=jnp.int32)[None, :]).astype(
        jnp.int32
    )
    before = jnp.cumsum(owner_hot, axis=0) - owner_hot
    slot_rank = jnp.sum(before * owner_hot, axis=1)
    slot_index = owner_index * capacity + slot_rank
    request = jnp.full((slot_count,), -1, jnp.int32).at[slot_index].set(local_row)
    asked_rows = lax.all_to_all(
        request.reshape(groups, capacity), GRP, split_axis=0, concat_axis=0, tiled=True
    ).reshape(slot_count)
    present = asked_rows >= 0
    safe_rows = jnp.maximum(asked_rows, 0)
    slot_lengths = jnp.where(present, lengths[:, 0][safe_rows], 0)
    stored_index = jnp.arange(passage_local, dtype=jnp.int32)
    gather_hot = (asked_rows[None, :] == stored_index[:, None]).astype(jnp.bfloat16)
    pick_hot = (asked_rows[:, None] == stored_index[None, :]).astype(jnp.bfloat16)
    route_hot = (slot_index[:, None] == jnp.arange(slot_count, dtype=jnp.int32)[None, :]).astype(
        jnp.bfloat16
    )
    flat_passages = passages.reshape(passage_local, block_width)
    query_flat = queries[:, 0]
    query_weights = weights[:, 0]
    query_source = jnp.arange(ref_count, dtype=jnp.int32) // candidates
    blocks_flat = jnp.dot(pick_hot, flat_passages, preferred_element_type=jnp.float32).astype(
        jnp.bfloat16
    )
    ref_queries = query_flat[query_source].reshape(ref_count, query_width)
    slot_queries = jnp.einsum(
        "rs,rk->sk", route_hot, ref_queries, preferred_element_type=jnp.float32
    ).astype(jnp.bfloat16)
    got_queries = lax.all_to_all(
        slot_queries.reshape(groups, capacity, query_width),
        GRP,
        split_axis=0,
        concat_axis=0,
        tiled=True,
    )
    got_queries = got_queries.reshape(slot_count, query_len, feature_dim)
    blocks = blocks_flat.reshape(slot_count, token_len, feature_dim)
    products = jnp.einsum("sid,sjd->sij", got_queries, blocks, preferred_element_type=jnp.float32)
    matched, attention = token_softmax(products, jnp.maximum(slot_lengths, 1))
    slot_scores = jnp.sum(matched, axis=-1)
    back_scores = lax.all_to_all(
        slot_scores.reshape(groups, capacity), GRP, split_axis=0, concat_axis=0, tiled=True
    ).reshape(slot_count)
    student = back_scores[slot_index].reshape(query_local, candidates)
    log_student = jax.nn.log_softmax(student, axis=-1)
    log_teacher = jax.nn.log_softmax(teacher[:, 0], axis=-1)
    teacher_prob = jnp.exp(log_teacher)
    divergence = jnp.sum(teacher_prob * (log_teacher - log_student), axis=-1)
    totals = (
        over_axes(jnp.sum(query_weights * divergence), GRP_REP),
        over_axes(jnp.sum(query_weights), GRP_REP),
    )
    loss_value = totals[0] / totals[1]
    scale_all = query_local * groups * replicas
    score_grad = (
        scale_all * query_weights[:, None] / totals[1] * (jnp.exp(log_student) - teacher_prob)
    )
    loss_value, score_grad = (loss_value, score_grad)
    slot_score_grad = (
        jnp.zeros((slot_count,), jnp.float32).at[slot_index].set(score_grad.reshape(ref_count))
    )
    arrived = lax.all_to_all(
        slot_score_grad.reshape(groups, capacity), GRP, split_axis=0, concat_axis=0, tiled=True
    ).reshape(slot_count)
    scaled_grad = (arrived[:, None, None] * attention).astype(jnp.bfloat16)
    pair_query = jnp.einsum(
        "sij,sjd->sid", scaled_grad, blocks, preferred_element_type=jnp.float32
    ).astype(jnp.bfloat16)
    returned_queries = lax.all_to_all(
        pair_query.reshape(groups, capacity, query_width),
        GRP,
        split_axis=0,
        concat_axis=0,
        tiled=True,
    )
    ordered = jnp.dot(
        route_hot,
        returned_queries.reshape(slot_count, query_width),
        preferred_element_type=jnp.float32,
    )
    query_grad = jnp.sum(ordered.reshape(query_local, candidates, query_len, feature_dim), axis=1)
    returned = jnp.einsum(
        "sij,sid->sjd", scaled_grad, got_queries, preferred_element_type=jnp.float32
    ).astype(jnp.bfloat16)
    returned = returned.reshape(slot_count, block_width)
    passage_sum = jnp.dot(gather_hot, returned, preferred_element_type=jnp.float32)
    passage_grad = passage_sum.astype(jnp.bfloat16).reshape(
        passage_local, 1, token_len, feature_dim
    )
    return (loss_value, query_grad[:, None], passage_grad)


def solution(mesh):
    finer = Mesh(mesh.devices.reshape(8, 4, 4, 2), ("grp_0", "grp_1", "rep_0", "rep_1"))
    in_specs = (
        P(GRP, REP, None, None),
        P(GRP, REP, None, None),
        P(GRP, REP),
        P(GRP, REP, None),
        P(REP, None),
        P(GRP, REP, None),
        P(GRP, REP),
    )
    out_specs = (P(), P(GRP, REP, None, None), P(GRP, REP, None, None))
    return jax.shard_map(
        on_device, mesh=finer, in_specs=in_specs, out_specs=out_specs, check_vma=False
    )
```

profile of v0, /device:TPU:8, one launch (start us, length us, event | category | flops | bytes accessed | tf_op | source)
XLA Modules:
  0.0 256.7 jit_solution(11497343918002270158)
XLA Ops:
  0.7 0.5 broadcast.316
  1.2 1.3 reduce.17
  2.5 0.1 eq.91
  2.6 1.0 select_reduce_fusion
  3.6 0.1 fusion.12
  3.7 0.2 reduce_window_sum.11
  3.9 0.2 select_reduce_fusion.1
  4.1 1.0 scatter_custom_fusion
  5.0 0.7 all_to_all.24
  5.7 11.7 %all-to-all-start = ((s32[32,1,8]{2,1,0:T(1,128)}), s32[32,1,8]{2,1,0:T(1,128)S(1)}, u32[]{:S(2)}, u32[]{:S(2)}) async-start(s32[32,1,8]{2,1,0:T(1,128)} %bitcast.6), calls=%async_computation | async-start | bytes 32768 | tf_op jit(solution)/shard_map/all_to_all | solution.py:61
  17.5 0.8 gather_fusion.1
  18.3 2.2 fusion.1
  20.4 5.5 %all-to-all-done = s32[32,1,8]{2,1,0:T(1,128)S(1)} async-done(((s32[32,1,8]{2,1,0:T(1,128)}), s32[32,1,8]{2,1,0:T(1,128)S(1)}, u32[]{:S(2)}, u32[]{:S(2)}) %all-to-all-start) | async-done | bytes 1056 | tf_op jit(solution)/shard_map/all_to_all | solution.py:61
  25.9 5.8 %all-to-all-start.1 = ((bf16[32,8,4096]{2,1,0:T(8,128)(2,1)}), bf16[32,8,4096]{2,1,0:T(8,128)(2,1)}, u32[]{:S(2)}, u32[]{:S(2)}) async-start(bf16[32,8,4096]{2,1,0:T(8,128)(2,1)} %fusion.1), calls=%async_computation.1 | async-start | bytes 4194304 | tf_op jit(solution)/shard_map/all_to_all | solution.py:84
  31.7 3.7 %copy.30 = bf16[64,1,180,128]{3,2,0,1:T(8,128)(2,1)S(1)} copy(bf16[64,1,180,128]{3,0,2,1:T(8,128)(2,1)} %param.9) | data formatting | bytes 5898240 | tf_op args[1]
  35.5 0.1 reduce_max.23
  35.6 0.2 exponential_reduce_fusion.1
  35.8 0.7 maximum_reduce_fusion
  36.5 0.1 reshape.254
  36.6 0.1 reshape.239
  36.7 6.2 %convolution_convert_fusion = bf16[256,23040]{1,0:T(8,128)(2,1)} fusion(bf16[8,8,180,128]{3,2,1,0:T(8,128)(2,1)S(1)} %bitcast.71, s32[256]{0:T(256)S(1)} %reshape.239), kind=kOutput, calls=%fused_computation.5 | convolution fusion | flops 760889344 | bytes 14746624 | tf_op jit(solution)/shard_map/dot_general | solution.py:77
  42.9 16.2 %copy.31 = bf16[256,23040]{0,1:T(8,128)(2,1)} copy(bf16[256,23040]{1,0:T(8,128)(2,1)} %convolution_convert_fusion) | data formatting | bytes 23592960 | tf_op jit(solution)/shard_map/convert_element_type | solution.py:77
  59.1 16.5 %copy.32 = bf16[256,180,128]{2,1,0:T(8,128)(2,1)} copy(bf16[256,180,128]{0,2,1:T(8,128)(2,1)} %bitcast.70) | data formatting | bytes 23592960 | tf_op jit(solution)/shard_map/reshape | solution.py:92
  75.7 1.9 gather_fusion
  77.6 2.8 %all-to-all-done.1 = bf16[32,8,4096]{2,1,0:T(8,128)(2,1)} async-done(((bf16[32,8,4096]{2,1,0:T(8,128)(2,1)}), bf16[32,8,4096]{2,1,0:T(8,128)(2,1)}, u32[]{:S(2)}, u32[]{:S(2)}) %all-to-all-start.1) | async-done | bytes 2097184 | tf_op jit(solution)/shard_map/all_to_all | solution.py:84
  80.3 2.1 copy.41
  82.4 15.2 %fusion = (f32[256,32]{1,0:T(8,128)S(1)}, f32[256,32,180]{2,1,0:T(8,128)}) fusion(s32[256]{0:T(256)S(1)} %fusion.14, bf16[256,32,128]{2,1,0:T(8,128)(2,1)S(1)} %bitcast.73, bf16[256,180,128]{2,1,0:T(8,128)(2,1)} %copy.32), kind=kOutput, calls=%fused_computation.12 | convolution fusion | flops 383377408 | bytes 19825664 | tf_op jit(solution)/shard_map/sid,sjd->sij/dot_general | solution.py:93
  97.7 6.4 %fusion.2 = f32[256,32]{1,0:T(8,128)S(1)} fusion(f32[256,32,180]{2,1,0:T(8,128)} %get-tuple-element.29, f32[256,32]{1,0:T(8,128)S(1)} %get-tuple-element.28, s32[256]{0:T(256)S(1)} %fusion.14), kind=kLoop, calls=%fused_computation.15 | loop fusion | flops 8839168 | bytes 5964800 | tf_op jit(solution)/shard_map/reduce_sum | solution.py:27
  104.1 0.1 multiply_reduce_fusion
  104.2 0.7 all_to_all.27
  104.9 7.1 %all-to-all-start.2 = ((f32[32,1,8]{2,1,0:T(1,128)}), f32[32,1,8]{2,1,0:T(1,128)S(1)}, u32[]{:S(2)}, u32[]{:S(2)}) async-start(f32[32,1,8]{2,1,0:T(1,128)} %bitcast.12), calls=%async_computation.2 | async-start | bytes 32768 | tf_op jit(solution)/shard_map/all_to_all | solution.py:96
  112.1 0.6 reduce_sum.97
  112.7 7.8 %all-to-all-done.2 = f32[32,1,8]{2,1,0:T(1,128)S(1)} async-done(((f32[32,1,8]{2,1,0:T(1,128)}), f32[32,1,8]{2,1,0:T(1,128)S(1)}, u32[]{:S(2)}, u32[]{:S(2)}) %all-to-all-start.2) | async-done | bytes 1056 | tf_op jit(solution)/shard_map/all_to_all | solution.py:96
  120.5 0.5 broadcast.318
  121.0 0.7 reduce.19
  121.7 0.1 reshape.245
  121.8 1.3 gather_fusion.2
  123.1 0.1 reshape.246
  123.2 0.1 reduce_max.24
  123.3 0.2 exponential_reduce_fusion
  123.5 0.2 multiply_reduce_fusion.1
  123.7 0.6 fusion.17
  124.3 15.4 %all-reduce = (f32[]{:T(128)}, f32[]{:T(128)}) all-reduce(f32[]{:T(128)} %fusion.17, f32[]{:T(128)} %reduce_sum.97), channel_id=1, replica_groups=mesh['grp_0'=8,'grp_1'=4,'rep_0'=4,'rep_1'=2] {'grp_0'}, use_global_device_ids=true, to_apply=%region_11.13 | all-reduce | flops 2 | bytes 16 | tf_op jit(solution)/shard_map/psum | solution.py:15
  139.7 9.9 %all-reduce.2 = (f32[]{:T(128)}, f32[]{:T(128)}) all-reduce(f32[]{:T(128)} %get-tuple-element.18, f32[]{:T(128)} %get-tuple-element.19), channel_id=1, replica_groups=mesh['grp_0'=8,'grp_1'=4,'rep_0'=4,'rep_1'=2] {'grp_1'}, use_global_device_ids=true, to_apply=%region_12.14 | all-reduce | flops 2 | bytes 16 | tf_op jit(solution)/shard_map/psum | solution.py:15
  149.5 11.0 %all-reduce.1 = (f32[]{:T(128)}, f32[]{:T(128)}) all-reduce(f32[]{:T(128)} %get-tuple-element.22, f32[]{:T(128)} %get-tuple-element.23), channel_id=1, replica_groups=mesh['grp_0'=8,'grp_1'=4,'rep_0'=4,'rep_1'=2] {'rep_0'}, use_global_device_ids=true, to_apply=%region_13.15 | all-reduce | flops 2 | bytes 16 | tf_op jit(solution)/shard_map/psum | solution.py:15
  160.6 3.4 %all-reduce.3 = (f32[]{:T(128)}, f32[]{:T(128)}) all-reduce(f32[]{:T(128)} %get-tuple-element.20, f32[]{:T(128)} %get-tuple-element.21), channel_id=1, replica_groups=mesh['grp_0'=8,'grp_1'=4,'rep_0'=4,'rep_1'=2] {'rep_1'}, use_global_device_ids=true, to_apply=%region_14.16 | all-reduce | flops 2 | bytes 16 | tf_op jit(solution)/shard_map/psum | solution.py:15
  164.0 0.7 divide_bitcast_fusion
  164.7 0.1 reshape.288
  164.8 1.0 scatter_custom_fusion.1
  165.9 14.0 %all_to_all.37 = f32[32,1,8]{2,1,0:T(1,128)S(1)} all-to-all(f32[32,1,8]{2,1,0:T(1,128)S(1)} %bitcast.76), channel_id=1, replica_groups=mesh['grp_0'=8,'grp_1'=4,'rep_0'=4,'rep_1'=2] {'grp_0','grp_1'}, dimensions={0} | all-to-all | bytes 2048 | tf_op jit(solution)/shard_map/all_to_all | solution.py:117
  179.9 0.7 reduce.20
  180.6 0.1 mul.78
  180.7 10.3 %convolution_convert_fusion.4 = bf16[256,32,128]{2,1,0:T(8,128)(2,1)} fusion(bf16[256,180,128]{2,1,0:T(8,128)(2,1)} %copy.32, f32[256,32,180]{2,1,0:T(8,128)} %get-tuple-element.29, f32[256,32]{1,0:T(8,128)S(1)} %fusion.2, f32[256]{0:T(256)S(1)} %mul.78, f32[256,32]{1,0:T(8,128)S(1)} %get-tuple-element.28, s32[256]{0:T(256)S(1)} %fusion.14), kind=kOutput, calls=%fused_computation.18 | convolution fusion | flops 390332416 | bytes 19859456 | tf_op jit(solution)/shard_map/sij,sjd->sid/dot_general | solution.py:121
  191.0 4.2 %reshape.248 = bf16[32,8,4096]{2,1,0:T(8,128)(2,1)} reshape(bf16[256,32,128]{2,1,0:T(8,128)(2,1)} %convolution_convert_fusion.4) | data formatting | bytes 4194304 | tf_op jit(solution)/shard_map/reshape | solution.py:125
  195.2 5.8 %all-to-all-start.4 = ((bf16[32,8,4096]{2,1,0:T(8,128)(2,1)}), bf16[32,8,4096]{2,1,0:T(8,128)(2,1)}, u32[]{:S(2)}, u32[]{:S(2)}) async-start(bf16[32,8,4096]{2,1,0:T(8,128)(2,1)} %reshape.248), calls=%async_computation.4 | async-start | bytes 4194304 | tf_op jit(solution)/shard_map/all_to_all | solution.py:124
  200.9 0.1 reduce_sum.99
  202.5 14.7 %convolution_convert_fusion.2 = bf16[256,180,128]{2,1,0:T(8,128)(2,1)} fusion(bf16[256,32,128]{2,1,0:T(8,128)(2,1)S(1)} %bitcast.74, f32[256,32,180]{2,1,0:T(8,128)} %get-tuple-element.29, f32[256,32]{1,0:T(8,128)S(1)} %fusion.2, f32[256]{0:T(256)S(1)} %mul.78, f32[256,32]{1,0:T(8,128)S(1)} %get-tuple-element.28, s32[256]{0:T(256)S(1)} %fusion.14), kind=kOutput, calls=%fused_computation.11 | convolution fusion | flops 395182080 | bytes 19859456 | tf_op jit(solution)/shard_map/sij,sid->sjd/dot_general | solution.py:137
  217.2 16.4 %copy.37 = bf16[256,180,128]{0,2,1:T(8,128)(2,1)} copy(bf16[256,180,128]{2,1,0:T(8,128)(2,1)} %convolution_convert_fusion.2) | data formatting | bytes 23592960 | tf_op jit(solution)/shard_map/convert_element_type | solution.py:139
  233.6 8.0 %convolution_convert_fusion.1 = bf16[64,23040]{1,0:T(8,128)(2,1)S(1)} fusion(bf16[256,23040]{0,1:T(8,128)(2,1)} %bitcast.69, s32[256]{0:T(256)S(1)} %reshape.239), kind=kOutput, calls=%fused_computation.6 | convolution fusion | flops 756465664 | bytes 14746624 | tf_op jit(solution)/shard_map/dot_general | solution.py:141
  241.6 2.9 %reshape.251 = bf16[64,1,180,128]{3,2,0,1:T(8,128)(2,1)} reshape(bf16[64,23040]{1,0:T(8,128)(2,1)S(1)} %convolution_convert_fusion.1) | data formatting | bytes 5898240 | tf_op jit(solution)/shard_map/reshape | solution.py:142
  244.5 4.2 %copy.38 = bf16[64,1,180,128]{3,0,2,1:T(8,128)(2,1)} copy(bf16[64,1,180,128]{3,2,0,1:T(8,128)(2,1)} %reshape.251) | data formatting | bytes 5898240
  248.7 2.1 all-to-all-done.4
  250.8 3.3 %copy.36 = bf16[256,4096]{0,1:T(8,128)(2,1)S(1)} copy(bf16[256,4096]{1,0:T(8,128)(2,1)} %bitcast.18) | data formatting | bytes 4194304 | tf_op jit(solution)/shard_map/reshape | solution.py:133
  254.1 1.4 convolution_reduce_fusion
  (24 shorter events, 0.4 us)
Async XLA Ops:
  0.6 16.9 %copy-start = (bf16[2,1,32,128]{3,2,1,0:T(8,128)(2,1)S(1)}, bf16[2,1,32,128]{3,2,1,0:T(8,128)(2,1)}, u32[]{:S(2)}) copy-start(bf16[2,1,32,128]{3,2,1,0:T(8,128)(2,1)} %param.8) | copy-start | bytes 49156
  0.6 34.8 %copy-start.3 = (f32[2,1,64]{2,1,0:T(1,128)S(1)}, f32[2,1,64]{2,1,0:T(1,128)}, u32[]{:S(2)}) copy-start(f32[2,1,64]{2,1,0:T(1,128)} %param.13) | copy-start | bytes 1540
  5.7 20.2 %all-to-all-start = ((s32[32,1,8]{2,1,0:T(1,128)}), s32[32,1,8]{2,1,0:T(1,128)S(1)}, u32[]{:S(2)}, u32[]{:S(2)}) async-start(s32[32,1,8]{2,1,0:T(1,128)} %bitcast.6), calls=%async_computation | async-start | bytes 32768 | tf_op jit(solution)/shard_map/all_to_all | solution.py:61
  25.9 54.4 %all-to-all-start.1 = ((bf16[32,8,4096]{2,1,0:T(8,128)(2,1)}), bf16[32,8,4096]{2,1,0:T(8,128)(2,1)}, u32[]{:S(2)}, u32[]{:S(2)}) async-start(bf16[32,8,4096]{2,1,0:T(8,128)(2,1)} %fusion.1), calls=%async_computation.1 | async-start | bytes 4194304 | tf_op jit(solution)/shard_map/all_to_all | solution.py:84
  59.1 16.5 %copy-start.2 = (s32[64,1]{0,1:T(1,128)S(1)}, s32[64,1]{0,1:T(1,128)}, u32[]{:S(2)}) copy-start(s32[64,1]{0,1:T(1,128)} %param.10) | copy-start | bytes 772
  97.6 14.4 %copy-start.4 = (f32[2,1]{0,1:T(1,128)S(1)}, f32[2,1]{0,1:T(1,128)}, u32[]{:S(2)}) copy-start(f32[2,1]{0,1:T(1,128)} %param.14) | copy-start | bytes 28
  104.9 15.6 %all-to-all-start.2 = ((f32[32,1,8]{2,1,0:T(1,128)}), f32[32,1,8]{2,1,0:T(1,128)S(1)}, u32[]{:S(2)}, u32[]{:S(2)}) async-start(f32[32,1,8]{2,1,0:T(1,128)} %bitcast.12), calls=%async_computation.2 | async-start | bytes 32768 | tf_op jit(solution)/shard_map/all_to_all | solution.py:96
  195.2 55.6 %all-to-all-start.4 = ((bf16[32,8,4096]{2,1,0:T(8,128)(2,1)}), bf16[32,8,4096]{2,1,0:T(8,128)(2,1)}, u32[]{:S(2)}, u32[]{:S(2)}) async-start(bf16[32,8,4096]{2,1,0:T(8,128)(2,1)} %reshape.248), calls=%async_computation.4 | async-start | bytes 4194304 | tf_op jit(solution)/shard_map/all_to_all | solution.py:124
  233.6 21.9 %copy-start.1 = (bf16[2,1,32,128]{3,2,1,0:T(8,128)(2,1)S(1)}, bf16[2,1,32,128]{3,2,1,0:T(8,128)(2,1)}, u32[]{:S(2)}) copy-start(bf16[2,1,32,128]{3,2,1,0:T(8,128)(2,1)} %param.8) | copy-start | bytes 49156
where the time goes:
time: 259 us; the launch traced here: 257 us
  local copies, waits for them, and re-layouts  78.7 us (30%)
  matrix products  58 us (22%)
  blocking collectives  53.7 us (21%)
  starting transfers between devices  30.4 us (12%)
  waiting for transfers between devices  18.2 us (7%)
  other arithmetic  14.3 us (6%)
  between operations  3.42 us (1%)
    psum x4, blocking collectives, over_axes(): shard = lax.psum(shard, axis)  39.6 us
    reshape x1, local copies, waits for them, and re-layouts, on_device(): blocks = blocks_flat.reshape(slot_count, token_len, feature_dim)  16.5 us
    convert_element_type x1, local copies, waits for them, and re-layouts, on_device(): returned = jnp.einsum('sij,sid->sjd', scaled_grad, got_queries, preferred...  16.4 us
    convert_element_type x1, local copies, waits for them, and re-layouts, on_device(): jnp.dot(pick_hot, flat_passages, preferred_element_type=jnp.float32)  16.2 us
    dot_general x1, matrix products, on_device(): jnp.einsum('sid,sjd->sij', got_queries, blocks, preferred_element_type=jn...  15.2 us
    dot_general x1, matrix products, on_device(): jnp.einsum('sij,sid->sjd', scaled_grad, got_queries, preferred_element_ty...  14.7 us
    all_to_all x1, blocking collectives, on_device(): lax.all_to_all(slot_score_grad.reshape(groups, capacity), GRP, split_axis...  14 us
    all_to_all x1, starting transfers between devices, on_device(): lax.all_to_all(request.reshape(groups, capacity), GRP, split_axis=0, conc...  11.7 us
  transfers between devices with their start and end apart: 4, of which 4 were waited for; matrix products, arithmetic and copies ran while one was open for 37% of the time, Pallas kernels for 0%

commit v1 on v0

--- a/solution.py
+++ b/solution.py
@@ -12,7 +12,7 @@
 
 def over_axes(shard, axes):
     for axis in axes:
-        shard = lax.psum(shard, axis)
+        shard = jnp.sum(jax.lax.all_gather(shard, axis), axis=0)
     return shard
 
 

time: 259 us -> 272 us (1.050)
  local copies, waits for them, and re-layouts: 78.7 us -> 92.5 us
  other arithmetic: 14.3 us -> 19.3 us
  blocking collectives: 53.7 us -> 50.8 us
    psum x4 -> x0, blocking collectives: 39.6 us -> none  [over_axes(): shard = lax.psum(shard, axis)]
    unnamed x0 -> x4, blocking collectives: none -> 36.8 us
    unnamed x14 -> x42, local copies, waits for them, and re-layouts: 10.6 us -> 24.4 us
    reduce_sum x0 -> x8, other arithmetic: none -> 5.05 us  [over_axes(): shard = jnp.sum(jax.lax.all_gather(shard, axis), axis=0)]
  transfers between devices with their start and end apart: 4 -> 4, of which waited for: 4 -> 4; matrix products, arithmetic and copies ran while one was open for 37% -> 36% of each run, Pallas kernels for 0% -> 0%
where the time goes in v1:
time: 272 us; the launch traced here: 270 us
  local copies, waits for them, and re-layouts  92.5 us (34%)
  matrix products  58 us (21%)
  blocking collectives  50.8 us (19%)
  starting transfers between devices  30.4 us (11%)
  other arithmetic  19.3 us (7%)
  waiting for transfers between devices  15.6 us (6%)
  between operations  3.44 us (1%)
    unnamed x4, blocking collectives  36.8 us
    unnamed x42, local copies, waits for them, and re-layouts  24.4 us
    reshape x1, local copies, waits for them, and re-layouts, on_device(): blocks = blocks_flat.reshape(slot_count, token_len, feature_dim)  16.5 us
    convert_element_type x1, local copies, waits for them, and re-layouts, on_device(): returned = jnp.einsum('sij,sid->sjd', scaled_grad, got_queries, preferred...  16.4 us
    convert_element_type x1, local copies, waits for them, and re-layouts, on_device(): jnp.dot(pick_hot, flat_passages, preferred_element_type=jnp.float32)  16.2 us
    dot_general x1, matrix products, on_device(): jnp.einsum('sid,sjd->sij', got_queries, blocks, preferred_element_type=jn...  15.2 us
    dot_general x1, matrix products, on_device(): jnp.einsum('sij,sid->sjd', scaled_grad, got_queries, preferred_element_ty...  14.7 us
    all_to_all x1, blocking collectives, on_device(): lax.all_to_all(slot_score_grad.reshape(groups, capacity), GRP, split_axis...  14 us
  transfers between devices with their start and end apart: 4, of which 4 were waited for; matrix products, arithmetic and copies ran while one was open for 36% of the time, Pallas kernels for 0%

profile of v1, /device:TPU:8, one launch (start us, length us, event | category | flops | bytes accessed | tf_op | source)
XLA Modules:
  0.0 270.1 jit_solution(5656412660040730990)
XLA Ops:
  1.2 1.3 reduce.25
  2.6 1.0 select_reduce_fusion
  4.1 1.0 scatter_custom_fusion
  5.0 0.7 all_to_all.24
  5.7 11.7 %all-to-all-start = ((s32[32,1,8]{2,1,0:T(1,128)}), s32[32,1,8]{2,1,0:T(1,128)S(1)}, u32[]{:S(2)}, u32[]{:S(2)}) async-start(s32[32,1,8]{2,1,0:T(1,128)} %bitcast.6), calls=%async_computation | async-start | bytes 32768 | tf_op jit(solution)/shard_map/all_to_all | solution.py:61
  17.5 0.8 gather_fusion.1
  18.3 2.2 fusion.1
  20.4 5.5 %all-to-all-done = s32[32,1,8]{2,1,0:T(1,128)S(1)} async-done(((s32[32,1,8]{2,1,0:T(1,128)}), s32[32,1,8]{2,1,0:T(1,128)S(1)}, u32[]{:S(2)}, u32[]{:S(2)}) %all-to-all-start) | async-done | bytes 1056 | tf_op jit(solution)/shard_map/all_to_all | solution.py:61
  25.9 5.8 %all-to-all-start.1 = ((bf16[32,8,4096]{2,1,0:T(8,128)(2,1)}), bf16[32,8,4096]{2,1,0:T(8,128)(2,1)}, u32[]{:S(2)}, u32[]{:S(2)}) async-start(bf16[32,8,4096]{2,1,0:T(8,128)(2,1)} %fusion.1), calls=%async_computation.1 | async-start | bytes 4194304 | tf_op jit(solution)/shard_map/all_to_all | solution.py:84
  31.7 3.7 %copy.30 = bf16[64,1,180,128]{3,2,0,1:T(8,128)(2,1)S(1)} copy(bf16[64,1,180,128]{3,0,2,1:T(8,128)(2,1)} %param.9) | data formatting | bytes 5898240 | tf_op args[1]
  35.8 0.7 maximum_reduce_fusion
  36.7 6.2 %convolution_convert_fusion = bf16[256,23040]{1,0:T(8,128)(2,1)} fusion(bf16[8,8,180,128]{3,2,1,0:T(8,128)(2,1)S(1)} %bitcast.83, s32[256]{0:T(256)S(1)} %reshape.239), kind=kOutput, calls=%fused_computation.5 | convolution fusion | flops 760889344 | bytes 14746624 | tf_op jit(solution)/shard_map/dot_general | solution.py:77
  42.9 16.2 %copy.31 = bf16[256,23040]{0,1:T(8,128)(2,1)} copy(bf16[256,23040]{1,0:T(8,128)(2,1)} %convolution_convert_fusion) | data formatting | bytes 23592960 | tf_op jit(solution)/shard_map/convert_element_type | solution.py:77
  59.1 16.5 %copy.32 = bf16[256,180,128]{2,1,0:T(8,128)(2,1)} copy(bf16[256,180,128]{0,2,1:T(8,128)(2,1)} %bitcast.82) | data formatting | bytes 23592960 | tf_op jit(solution)/shard_map/reshape | solution.py:92
  75.7 1.9 gather_fusion
  77.6 2.8 %all-to-all-done.1 = bf16[32,8,4096]{2,1,0:T(8,128)(2,1)} async-done(((bf16[32,8,4096]{2,1,0:T(8,128)(2,1)}), bf16[32,8,4096]{2,1,0:T(8,128)(2,1)}, u32[]{:S(2)}, u32[]{:S(2)}) %all-to-all-start.1) | async-done | bytes 2097184 | tf_op jit(solution)/shard_map/all_to_all | solution.py:84
  80.3 2.1 copy.41
  82.4 15.2 %fusion = (f32[256,32]{1,0:T(8,128)S(1)}, f32[256,32,180]{2,1,0:T(8,128)}) fusion(s32[256]{0:T(256)S(1)} %fusion.14, bf16[256,32,128]{2,1,0:T(8,128)(2,1)S(1)} %bitcast.85, bf16[256,180,128]{2,1,0:T(8,128)(2,1)} %copy.32), kind=kOutput, calls=%fused_computation.12 | convolution fusion | flops 383377408 | bytes 19825664 | tf_op jit(solution)/shard_map/sid,sjd->sij/dot_general | solution.py:93
  97.7 6.5 %fusion.2 = f32[256,32]{1,0:T(8,128)S(1)} fusion(f32[256,32,180]{2,1,0:T(8,128)} %get-tuple-element.29, f32[256,32]{1,0:T(8,128)S(1)} %get-tuple-element.28, s32[256]{0:T(256)S(1)} %fusion.14), kind=kLoop, calls=%fused_computation.15 | loop fusion | flops 8839168 | bytes 5964800 | tf_op jit(solution)/shard_map/reduce_sum | solution.py:27
  104.3 0.7 all_to_all.27
  105.0 7.1 %all-to-all-start.2 = ((f32[32,1,8]{2,1,0:T(1,128)}), f32[32,1,8]{2,1,0:T(1,128)S(1)}, u32[]{:S(2)}, u32[]{:S(2)}) async-start(f32[32,1,8]{2,1,0:T(1,128)} %bitcast.12), calls=%async_computation.2 | async-start | bytes 32768 | tf_op jit(solution)/shard_map/all_to_all | solution.py:96
  112.2 0.6 dynamic-slice
  112.7 0.6 reduce_sum.173
  113.4 1.4 dynamic-update-slice.4
  114.8 5.8 %all-to-all-done.2 = f32[32,1,8]{2,1,0:T(1,128)S(1)} async-done(((f32[32,1,8]{2,1,0:T(1,128)}), f32[32,1,8]{2,1,0:T(1,128)S(1)}, u32[]{:S(2)}, u32[]{:S(2)}) %all-to-all-start.2) | async-done | bytes 1056 | tf_op jit(solution)/shard_map/all_to_all | solution.py:96
  121.1 0.7 reduce.27
  121.9 1.3 gather_fusion.2
  123.8 0.6 fusion.17
  124.4 1.5 dynamic-update-slice
  125.9 0.6 dynamic-slice.1
  126.5 14.7 %all-reduce.8 = (f32[8]{0:T(128)S(1)}, f32[8]{0:T(128)S(1)}) all-reduce(f32[8]{0:T(128)S(1)} %dynamic-update-slice, f32[8]{0:T(128)S(1)} %dynamic-update-slice.4), channel_id=1, replica_groups=mesh['grp_0'=8,'grp_1'=4,'rep_0'=4,'rep_1'=2] {'grp_0'}, use_global_device_ids=true, to_apply=%add | all-reduce | flops 16 | bytes 128
  141.3 0.6 reduce_sum.169
  141.9 0.7 reduce_sum.174
  142.5 1.4 dynamic-update-slice.1
  143.9 1.4 dynamic-update-slice.5
  145.4 0.6 dynamic-slice.2
  146.0 9.2 %all-reduce.10 = (f32[4]{0:T(128)S(1)}, f32[4]{0:T(128)S(1)}) all-reduce(f32[4]{0:T(128)S(1)} %dynamic-update-slice.1, f32[4]{0:T(128)S(1)} %dynamic-update-slice.5), channel_id=1, replica_groups=mesh['grp_0'=8,'grp_1'=4,'rep_0'=4,'rep_1'=2] {'grp_1'}, use_global_device_ids=true, to_apply=%add.1 | all-reduce | flops 8 | bytes 64
  155.2 0.6 reduce_sum.170
  155.8 0.7 reduce_sum.175
  156.5 1.4 dynamic-update-slice.2
  157.9 1.4 dynamic-update-slice.6
  159.9 10.4 %all-reduce.9 = (f32[4]{0:T(128)S(1)}, f32[4]{0:T(128)S(1)}) all-reduce(f32[4]{0:T(128)S(1)} %dynamic-update-slice.2, f32[4]{0:T(128)S(1)} %dynamic-update-slice.6), channel_id=1, replica_groups=mesh['grp_0'=8,'grp_1'=4,'rep_0'=4,'rep_1'=2] {'rep_0'}, use_global_device_ids=true, to_apply=%add.2 | all-reduce | flops 8 | bytes 64
  170.3 0.6 reduce_sum.171
  170.9 0.7 reduce_sum.176
  171.6 1.4 dynamic-update-slice.3
  173.0 1.4 dynamic-update-slice.7
  174.4 2.4 all-reduce.11
  176.9 0.6 reduce_sum.177
  177.5 0.6 divide_bitcast_fusion
  178.3 1.0 scatter_custom_fusion.1
  179.4 14.0 %all_to_all.37 = f32[32,1,8]{2,1,0:T(1,128)S(1)} all-to-all(f32[32,1,8]{2,1,0:T(1,128)S(1)} %bitcast.88), channel_id=1, replica_groups=mesh['grp_0'=8,'grp_1'=4,'rep_0'=4,'rep_1'=2] {'grp_0','grp_1'}, dimensions={0} | all-to-all | bytes 2048 | tf_op jit(solution)/shard_map/all_to_all | solution.py:117
  193.4 0.7 reduce.28
  194.2 10.3 %convolution_convert_fusion.4 = bf16[256,32,128]{2,1,0:T(8,128)(2,1)} fusion(bf16[256,180,128]{2,1,0:T(8,128)(2,1)} %copy.32, f32[256,32,180]{2,1,0:T(8,128)} %get-tuple-element.29, f32[256,32]{1,0:T(8,128)S(1)} %fusion.2, f32[256]{0:T(256)S(1)} %mul.78, f32[256,32]{1,0:T(8,128)S(1)} %get-tuple-element.28, s32[256]{0:T(256)S(1)} %fusion.14), kind=kOutput, calls=%fused_computation.18 | convolution fusion | flops 390332416 | bytes 19859456 | tf_op jit(solution)/shard_map/sij,sjd->sid/dot_general | solution.py:121
  204.5 4.2 %reshape.248 = bf16[32,8,4096]{2,1,0:T(8,128)(2,1)} reshape(bf16[256,32,128]{2,1,0:T(8,128)(2,1)} %convolution_convert_fusion.4) | data formatting | bytes 4194304 | tf_op jit(solution)/shard_map/reshape | solution.py:125
  208.7 5.8 %all-to-all-start.4 = ((bf16[32,8,4096]{2,1,0:T(8,128)(2,1)}), bf16[32,8,4096]{2,1,0:T(8,128)(2,1)}, u32[]{:S(2)}, u32[]{:S(2)}) async-start(bf16[32,8,4096]{2,1,0:T(8,128)(2,1)} %reshape.248), calls=%async_computation.4 | async-start | bytes 4194304 | tf_op jit(solution)/shard_map/all_to_all | solution.py:124
  214.6 0.6 reduce_sum.172
  216.6 14.7 %convolution_convert_fusion.2 = bf16[256,180,128]{2,1,0:T(8,128)(2,1)} fusion(bf16[256,32,128]{2,1,0:T(8,128)(2,1)S(1)} %bitcast.86, f32[256,32,180]{2,1,0:T(8,128)} %get-tuple-element.29, f32[256,32]{1,0:T(8,128)S(1)} %fusion.2, f32[256]{0:T(256)S(1)} %mul.78, f32[256,32]{1,0:T(8,128)S(1)} %get-tuple-element.28, s32[256]{0:T(256)S(1)} %fusion.14), kind=kOutput, calls=%fused_computation.11 | convolution fusion | flops 395182080 | bytes 19859456 | tf_op jit(solution)/shard_map/sij,sid->sjd/dot_general | solution.py:137
  231.2 16.4 %copy.37 = bf16[256,180,128]{0,2,1:T(8,128)(2,1)} copy(bf16[256,180,128]{2,1,0:T(8,128)(2,1)} %convolution_convert_fusion.2) | data formatting | bytes 23592960 | tf_op jit(solution)/shard_map/convert_element_type | solution.py:139
  247.6 8.0 %convolution_convert_fusion.1 = bf16[64,23040]{1,0:T(8,128)(2,1)S(1)} fusion(bf16[256,23040]{0,1:T(8,128)(2,1)} %bitcast.81, s32[256]{0:T(256)S(1)} %reshape.239), kind=kOutput, calls=%fused_computation.6 | convolution fusion | flops 756465664 | bytes 14746624 | tf_op jit(solution)/shard_map/dot_general | solution.py:141
  255.7 2.9 %reshape.251 = bf16[64,1,180,128]{3,2,0,1:T(8,128)(2,1)} reshape(bf16[64,23040]{1,0:T(8,128)(2,1)S(1)} %convolution_convert_fusion.1) | data formatting | bytes 5898240 | tf_op jit(solution)/shard_map/reshape | solution.py:142
  258.5 4.2 %copy.38 = bf16[64,1,180,128]{3,0,2,1:T(8,128)(2,1)} copy(bf16[64,1,180,128]{3,2,0,1:T(8,128)(2,1)} %reshape.251) | data formatting | bytes 5898240
  262.8 1.5 all-to-all-done.4
  264.3 3.3 %copy.36 = bf16[256,4096]{0,1:T(8,128)(2,1)S(1)} copy(bf16[256,4096]{1,0:T(8,128)(2,1)} %bitcast.30) | data formatting | bytes 4194304 | tf_op jit(solution)/shard_map/reshape | solution.py:133
  267.6 1.4 convolution_reduce_fusion
  (60 shorter events, 4.0 us)
Async XLA Ops:
  0.6 16.9 %copy-start = (bf16[2,1,32,128]{3,2,1,0:T(8,128)(2,1)S(1)}, bf16[2,1,32,128]{3,2,1,0:T(8,128)(2,1)}, u32[]{:S(2)}) copy-start(bf16[2,1,32,128]{3,2,1,0:T(8,128)(2,1)} %param.8) | copy-start | bytes 49156
  0.6 34.8 %copy-start.3 = (f32[2,1,64]{2,1,0:T(1,128)S(1)}, f32[2,1,64]{2,1,0:T(1,128)}, u32[]{:S(2)}) copy-start(f32[2,1,64]{2,1,0:T(1,128)} %param.13) | copy-start | bytes 1540
  5.7 20.2 %all-to-all-start = ((s32[32,1,8]{2,1,0:T(1,128)}), s32[32,1,8]{2,1,0:T(1,128)S(1)}, u32[]{:S(2)}, u32[]{:S(2)}) async-start(s32[32,1,8]{2,1,0:T(1,128)} %bitcast.6), calls=%async_computation | async-start | bytes 32768 | tf_op jit(solution)/shard_map/all_to_all | solution.py:61
  25.9 54.4 %all-to-all-start.1 = ((bf16[32,8,4096]{2,1,0:T(8,128)(2,1)}), bf16[32,8,4096]{2,1,0:T(8,128)(2,1)}, u32[]{:S(2)}, u32[]{:S(2)}) async-start(bf16[32,8,4096]{2,1,0:T(8,128)(2,1)} %fusion.1), calls=%async_computation.1 | async-start | bytes 4194304 | tf_op jit(solution)/shard_map/all_to_all | solution.py:84
  59.1 16.5 %copy-start.2 = (s32[64,1]{0,1:T(1,128)S(1)}, s32[64,1]{0,1:T(1,128)}, u32[]{:S(2)}) copy-start(s32[64,1]{0,1:T(1,128)} %param.10) | copy-start | bytes 772
  97.6 14.5 %copy-start.8 = (u32[256]{0:T(256)S(1)}, u32[256]{0:T(256)}, u32[]{:S(2)}) copy-start(u32[256]{0:T(256)} %constant.82) | copy-start | bytes 3076
  97.7 15.1 %copy-start.4 = (f32[2,1]{0,1:T(1,128)S(1)}, f32[2,1]{0,1:T(1,128)}, u32[]{:S(2)}) copy-start(f32[2,1]{0,1:T(1,128)} %param.14) | copy-start | bytes 28
  97.7 28.3 %copy-start.7 = (u32[256]{0:T(256)S(1)}, u32[256]{0:T(256)}, u32[]{:S(2)}) copy-start(u32[256]{0:T(256)} %constant.87) | copy-start | bytes 3076
  97.7 47.7 %copy-start.6 = (u32[256]{0:T(256)S(1)}, u32[256]{0:T(256)}, u32[]{:S(2)}) copy-start(u32[256]{0:T(256)} %constant.92) | copy-start | bytes 3076
  97.7 61.7 %copy-start.5 = (u32[256]{0:T(256)S(1)}, u32[256]{0:T(256)}, u32[]{:S(2)}) copy-start(u32[256]{0:T(256)} %constant.97) | copy-start | bytes 3076
  105.0 15.6 %all-to-all-start.2 = ((f32[32,1,8]{2,1,0:T(1,128)}), f32[32,1,8]{2,1,0:T(1,128)S(1)}, u32[]{:S(2)}, u32[]{:S(2)}) async-start(f32[32,1,8]{2,1,0:T(1,128)} %bitcast.12), calls=%async_computation.2 | async-start | bytes 32768 | tf_op jit(solution)/shard_map/all_to_all | solution.py:96
  208.7 55.6 %all-to-all-start.4 = ((bf16[32,8,4096]{2,1,0:T(8,128)(2,1)}), bf16[32,8,4096]{2,1,0:T(8,128)(2,1)}, u32[]{:S(2)}, u32[]{:S(2)}) async-start(bf16[32,8,4096]{2,1,0:T(8,128)(2,1)} %reshape.248), calls=%async_computation.4 | async-start | bytes 4194304 | tf_op jit(solution)/shard_map/all_to_all | solution.py:124
  247.6 21.4 %copy-start.1 = (bf16[2,1,32,128]{3,2,1,0:T(8,128)(2,1)S(1)}, bf16[2,1,32,128]{3,2,1,0:T(8,128)(2,1)}, u32[]{:S(2)}) copy-start(bf16[2,1,32,128]{3,2,1,0:T(8,128)(2,1)} %param.8) | copy-start | bytes 49156
